TPU v7x, 128 devices: a whole 4x4x4 slice. The times are simulated.
128 devices in a mesh: z: 4 (over z), y: 4 (over y), x: 8 (over x, core).
Axes of the slice: x: 4, y: 4, z: 4, core: 2. Of those that a mesh axis runs over, the one named last changes fastest.
Arguments:
- x_in: bfloat16 [131072, 2048], P(('z', 'y', 'x'))
- g_out: bfloat16 [131072, 256], P(('z', 'y', 'x'))
- w_in: bfloat16 [2048, 256], replicated
- w_up1: bfloat16 [256, 1024], replicated
- w_down1: bfloat16 [1024, 256], replicated
- w_up2: bfloat16 [256, 1024], replicated
- w_down2: bfloat16 [1024, 256], replicated
Outputs:
- output 1: bfloat16 [131072, 2048], P(('z', 'y', 'x'))
- output 2: float32 [2048, 256], replicated
- output 3: float32 [256, 1024], replicated
- output 4: float32 [1024, 256], replicated
- output 5: float32 [256, 1024], replicated
- output 6: float32 [1024, 256], replicated
All inputs are finite; a program needn't handle non-finite values.
Results may differ from a plain program's by a relative error of at most 0.0133384.
Values are sent between devices in bfloat16 or wider.
A program may use at most 1 GiB of HBM per device.

v0:
```python
import math
import jax
import jax.numpy as jnp
from jax import lax
from jax.sharding import PartitionSpec as P, NamedSharding

SQRT_HALF = 0.7071067811865476
INV_SQRT_TAU = 0.3989422804014327


def gelu_value(pre_act):
    pre_wide = pre_act.astype(jnp.float32)
    return 0.5 * pre_wide * (1.0 + lax.erf(pre_wide * SQRT_HALF))


def gelu_slope(pre_act):
    pre_wide = pre_act.astype(jnp.float32)
    return 0.5 * (1.0 + lax.erf(pre_wide * SQRT_HALF)) + pre_wide * jnp.exp(-0.5 * pre_wide * pre_wide) * INV_SQRT_TAU


def plain_product(first_op, second_op):
    return lax.dot_general(first_op, second_op, (((1,), (0,)), ((), ())), preferred_element_type=jnp.float32)


def rows_contract(first_op, second_op):
    return lax.dot_general(first_op, second_op, (((0,), (0,)), ((), ())), preferred_element_type=jnp.float32)


def times_transposed(first_op, second_op):
    return lax.dot_general(first_op, second_op, (((1,), (1,)), ((), ())), preferred_element_type=jnp.float32)


def solution(mesh):
    batch_axes = ("z", "y", "x")
    device_count = math.prod(mesh.shape.values())
    scale = 1.0 / device_count
    row_spec = P(batch_axes, None)
    full_spec = P(None, None)

    def mean_over_devices(grad):
        return lax.psum(grad, batch_axes) * scale

    def device_step(x_in, g_out, w_in, w_up1, w_down1, w_up2, w_down2):
        x_mid = plain_product(x_in, w_in).astype(jnp.bfloat16)
        pre_one = plain_product(x_mid, w_up1).astype(jnp.bfloat16)
        act_one = gelu_value(pre_one).astype(jnp.bfloat16)
        hid_two = (plain_product(act_one, w_down1) + x_mid.astype(jnp.float32)).astype(jnp.bfloat16)
        pre_three = plain_product(hid_two, w_up2).astype(jnp.bfloat16)
        act_three = gelu_value(pre_three).astype(jnp.bfloat16)
        dw_down2 = mean_over_devices(rows_contract(act_three, g_out))
        d_act3 = times_transposed(g_out, w_down2).astype(jnp.bfloat16)
        d_pre3 = (d_act3.astype(jnp.float32) * gelu_slope(pre_three)).astype(jnp.bfloat16)
        dw_up2 = mean_over_devices(rows_contract(hid_two, d_pre3))
        d_hid2 = (times_transposed(d_pre3, w_up2) + g_out.astype(jnp.float32)).astype(jnp.bfloat16)
        dw_down1 = mean_over_devices(rows_contract(act_one, d_hid2))
        d_act1 = times_transposed(d_hid2, w_down1).astype(jnp.bfloat16)
        d_pre1 = (d_act1.astype(jnp.float32) * gelu_slope(pre_one)).astype(jnp.bfloat16)
        dw_up1 = mean_over_devices(rows_contract(x_mid, d_pre1))
        d_mid = (times_transposed(d_pre1, w_up1) + d_hid2.astype(jnp.float32)).astype(jnp.bfloat16)
        dw_in = mean_over_devices(rows_contract(x_in, d_mid))
        dx_rows = times_transposed(d_mid, w_in).astype(jnp.bfloat16)
        return dx_rows, dw_in, dw_up1, dw_down1, dw_up2, dw_down2

    return jax.shard_map(
        device_step,
        mesh=mesh,
        in_specs=(row_spec, row_spec, full_spec, full_spec, full_spec, full_spec, full_spec),
        out_specs=(row_spec, full_spec, full_spec, full_spec, full_spec, full_spec),
        check_vma=False,
    )
```

profile of v0, /device:TPU:1, one launch (start us, length us, event | category | flops | bytes accessed | tf_op | source)
XLA Modules:
  0.0 208.7 jit_solution(10101639035694572036)
XLA Ops:
  7.2 0.0 copy-start
  7.2 0.0 copy-start.3
  7.2 0.0 all-reduce.3.cloned.1.call-start
  7.2 1.2 copy-done
  8.4 3.4 %convolution_convert_fusion.3 = bf16[1024,256]{1,0:T(8,128)(2,1)S(1)} fusion(bf16[1024,2048]{1,0:T(8,128)(2,1)} %param.7, bf16[2048,256]{1,0:T(8,128)(2,1)S(1)} %copy-done), kind=kOutput, calls=%fused_computation.40 | convolution fusion | flops 1074003968 | bytes 5767168 | tf_op jit(solution)/shard_map/dot_general | solution.py:22
  11.8 0.0 copy-done.3
  11.9 0.0 copy-start.5
  11.9 1.6 fusion.3
  13.5 0.0 copy-start.4
  13.5 0.0 copy-done.5
  13.5 0.0 copy-start.8
  13.5 0.8 fusion.21
  14.3 0.2 copy-done.4
  14.5 0.7 convolution_convert_fusion.1
  15.2 0.0 copy-done.8
  15.3 0.0 copy-start.7
  15.3 2.1 %fusion.18 = f32[1024,256]{1,0:T(8,128)} fusion(bf16[1024,256]{1,0:T(8,128)(2,1)S(1)} %copy-done.8, bf16[1024,1024]{1,0:T(8,128)(2,1)S(1)} %convolution_convert_fusion.1), kind=kOutput, calls=%fused_computation.30 | convolution fusion | flops 543162368 | bytes 3670016 | tf_op jit(solution)/shard_map/dot_general | solution.py:26
  17.4 0.0 copy-done.7
  17.4 2.3 %fusion.15 = bf16[1024,1024]{1,0:T(8,128)(2,1)S(1)} fusion(bf16[1024,1024]{1,0:T(8,128)(2,1)S(1)} %convolution_convert_fusion.1, bf16[1024,256]{1,0:T(8,128)(2,1)S(1)} %copy-done.8, bf16[1024,256]{1,0:T(8,128)(2,1)S(1)} %copy-done.7), kind=kOutput, calls=%fused_computation.25 | convolution fusion | flops 550502400 | bytes 5242880 | tf_op jit(solution)/shard_map/dot_general | solution.py:30
  19.6 0.8 fusion.22
  20.4 1.7 fusion.30
  22.1 1.8 fusion.25
  23.9 1.6 fusion.8
  25.5 0.0 copy-start.6
  25.5 0.8 fusion.23
  26.3 1.7 fusion.29
  28.0 0.0 copy-done.6
  28.0 2.6 %convolution_bitcast_fusion = f32[2048,256]{0,1:T(8,128)} fusion(bf16[1024,256]{1,0:T(8,128)(2,1)S(1)} %fusion.23, bf16[1024,2048]{1,0:T(8,128)(2,1)S(1)} %copy-done.6), kind=kOutput, calls=%fused_computation.29 | convolution fusion | flops 1073741824 | bytes 6815744 | tf_op jit(solution)/shard_map/dot_general | solution.py:26
  30.6 0.0 all-reduce.3.cloned.1.call-update
  30.6 3.3 %convolution_convert_fusion = bf16[1024,2048]{1,0:T(8,128)(2,1)} fusion(bf16[1024,256]{1,0:T(8,128)(2,1)S(1)} %fusion.23, bf16[2048,256]{1,0:T(8,128)(2,1)S(1)} %copy-done), kind=kOutput, calls=%fused_computation.28 | convolution fusion | flops 1075838976 | bytes 5767168 | tf_op jit(solution)/shard_map/dot_general | solution.py:30
  33.9 159.6 %all-reduce.3.cloned.1.call-done = (f32[2048,256]{0,1:T(8,128)}, f32[256,1024]{1,0:T(8,128)}, f32[1024,256]{1,0:T(8,128)}, f32[256,1024]{1,0:T(8,128)}, f32[1024,256]{1,0:T(8,128)}) async-done(((f32[2048,256]{0,1:T(8,128)}, f32[256,1024]{1,0:T(8,128)}, f32[1024,256]{1,0:T(8,128)}, f32[256,1024]{1,0:T(8,128)}, f32[1024,256]{1,0:T(8,128)}), (f32[2048,256]{0,1:T(8,128)}, f32[256,1024]{1,0:T(8,128)}, ...) | async-done | bytes 6291472 | tf_op jit(solution)/shard_map/psum | solution.py:41
  193.5 1.7 broadcast_multiply_fusion
  195.3 1.8 copy.13
  197.1 0.0 copy-start.1
  197.1 0.0 copy-start.2
  197.1 3.3 %broadcast_multiply_fusion.3 = (f32[256,1024]{1,0:T(8,128)}, f32[256,1024]{1,0:T(8,128)}) fusion(f32[256,1024]{1,0:T(8,128)} %get-tuple-element.15, f32[256,1024]{1,0:T(8,128)} %get-tuple-element.13), kind=kLoop, calls=%fused_computation.44 | loop fusion | flops 524288 | bytes 4194304 | tf_op jit(solution)/shard_map/mul | solution.py:41
  200.4 0.0 copy-done.1
  200.4 0.0 copy-done.2
  200.4 1.5 broadcast_multiply_fusion.1
Async XLA Ops:
  7.2 1.2 copy-start
  7.2 4.7 %copy-start.3 = (bf16[256,1024]{1,0:T(8,128)(2,1)S(1)}, bf16[256,1024]{1,0:T(8,128)(2,1)}, u32[]{:S(2)}) copy-start(bf16[256,1024]{1,0:T(8,128)(2,1)} %param.10) | copy-start | bytes 1572868
  7.2 186.3 %all-reduce.3.cloned.1.call-start = ((), (), s32[]{:S(2)}) async-start(), calls=%async_computation | async-start | bytes 12582912 | tf_op jit(solution)/shard_map/psum | solution.py:41
  11.9 1.6 copy-start.5
  13.5 1.0 copy-start.4
  13.5 1.7 copy-start.8
  15.3 2.1 %copy-start.7 = (bf16[1024,256]{1,0:T(8,128)(2,1)S(1)}, bf16[1024,256]{1,0:T(8,128)(2,1)}, u32[]{:S(2)}) copy-start(bf16[1024,256]{1,0:T(8,128)(2,1)} %param.13) | copy-start | bytes 1572868
  25.5 2.5 %copy-start.6 = (bf16[1024,2048]{1,0:T(8,128)(2,1)S(1)}, bf16[1024,2048]{1,0:T(8,128)(2,1)}, u32[]{:S(2)}) copy-start(bf16[1024,2048]{1,0:T(8,128)(2,1)} %param.7) | copy-start | bytes 12582916
  197.1 3.3 %copy-start.1 = (f32[1024,256]{1,0:T(8,128)S(1)}, f32[1024,256]{1,0:T(8,128)}, u32[]{:S(2)}) copy-start(f32[1024,256]{1,0:T(8,128)} %get-tuple-element.14) | copy-start | bytes 3145732
  197.1 3.3 %copy-start.2 = (f32[1024,256]{1,0:T(8,128)S(1)}, f32[1024,256]{1,0:T(8,128)}, u32[]{:S(2)}) copy-start(f32[1024,256]{1,0:T(8,128)} %get-tuple-element.16) | copy-start | bytes 3145732
Sparse Core Ops, SparseCore 0:
  30.7 162.7 all-reduce.2
where the time goes:
time: 209 us
  waiting for transfers between devices  160 us (77%)
  matrix products  25.1 us (12%)
  between operations  14.2 us (7%)
  other arithmetic  6.5 us (3%)
  local copies, waits for them, and re-layouts  3.24 us (2%)
    psum x1, waiting for transfers between devices, mean_over_devices(): return lax.psum(grad, batch_axes) * scale  160 us
    dot_general x5, matrix products, rows_contract(): lax.dot_general(first_op, second_op, (((0,), (0,)), ((), ())), preferred_...  9.93 us
    dot_general x5, matrix products, times_transposed(): lax.dot_general(first_op, second_op, (((1,), (1,)), ((), ())), preferred_...  8.66 us
    dot_general x4, matrix products, plain_product(): lax.dot_general(first_op, second_op, (((1,), (0,)), ((), ())), preferred_...  6.55 us
    mul x3, other arithmetic, mean_over_devices(): return lax.psum(grad, batch_axes) * scale  6.5 us
  transfers between devices with their start and end apart: 1, of which 1 were waited for; matrix products, arithmetic and copies ran while one was open for 2% of the time, Pallas kernels for 0%

commit v1 on v0

--- a/solution.py
+++ b/solution.py
@@ -2,10 +2,24 @@
 import jax
 import jax.numpy as jnp
 from jax import lax
-from jax.sharding import PartitionSpec as P, NamedSharding
+from jax.experimental import pallas as pl
+from jax.experimental.pallas import tpu as pltpu
+from jax.sharding import PartitionSpec as P
 
 SQRT_HALF = 0.7071067811865476
 INV_SQRT_TAU = 0.3989422804014327
+MESH = pl.DeviceIdType.MESH
+RING = 4
+UNITS = (
+    (0, 0, 1024, 256),
+    (1, 0, 256, 1024),
+    (2, 0, 1024, 256),
+    (3, 0, 256, 1024),
+    (4, 0, 1024, 256),
+    (4, 1024, 1024, 256),
+)
+SHAPES = ((1024, 256), (256, 1024), (1024, 256), (256, 1024), (2048, 256))
+ORDERS = (("x", "y", "z"), ("y", "z", "x"), ("z", "x", "y"))
 
 
 def gelu_value(pre_act):
@@ -28,6 +42,210 @@
 
 def times_transposed(first_op, second_op):
     return lax.dot_general(first_op, second_op, (((1,), (1,)), ((), ())), preferred_element_type=jnp.float32)
+
+
+def hinted(value, step):
+    return value if isinstance(value, int) else pl.multiple_of(value, step)
+
+
+class Region:
+    def __init__(self, row, rows, col, cols):
+        self.row, self.rows, self.col, self.cols = row, rows, col, cols
+
+    def at(self, ref):
+        return ref.at[pl.ds(hinted(self.row, 8), self.rows), pl.ds(hinted(self.col, 128), self.cols)]
+
+    def load(self, ref):
+        return ref[pl.ds(hinted(self.row, 8), self.rows), pl.ds(hinted(self.col, 128), self.cols)]
+
+    def store(self, ref, value):
+        ref[pl.ds(hinted(self.row, 8), self.rows), pl.ds(hinted(self.col, 128), self.cols)] = value
+
+    def part(self, index, count):
+        if self.rows // count >= 8:
+            step = self.rows // count
+            return Region(self.row + index * step, step, self.col, self.cols)
+        step = self.cols // count
+        return Region(self.row, self.rows, self.col + index * step, step)
+
+    def shape(self):
+        return (self.rows, self.cols)
+
+    def moved(self, row, col):
+        return Region(self.row + row, self.rows, self.col + col, self.cols)
+
+
+class Semaphores:
+    def __init__(self, send, recv):
+        self.send, self.recv, self.used, self.copies = send, recv, 0, []
+
+    def copy(self, source, target, device):
+        number = self.used
+        self.used += 1
+        made = pltpu.make_async_remote_copy(
+            src_ref=source,
+            dst_ref=target,
+            send_sem=self.send.at[number],
+            recv_sem=self.recv.at[number],
+            device_id=device,
+            device_id_type=MESH,
+        )
+        made.start()
+        self.copies.append(made)
+        return made
+
+
+def place():
+    x = lax.axis_index("x")
+    return {"x": x // 2, "y": lax.axis_index("y"), "z": lax.axis_index("z"), "core": lax.rem(x, 2)}
+
+
+def neighbour(here, axis, step):
+    other = lax.rem(here[axis] + step + RING, RING)
+    return {"x": other * 2 + here["core"]} if axis == "x" else {axis: other}
+
+
+def partner(here):
+    return {"x": here["x"] * 2 + 1 - here["core"]}
+
+
+def greet(here):
+    barrier = pltpu.get_barrier_semaphore()
+    peers = [partner(here)]
+    for axis in ("x", "y", "z"):
+        peers += [neighbour(here, axis, 1), neighbour(here, axis, -1)]
+    for peer in peers:
+        pl.semaphore_signal(barrier, inc=1, device_id=peer, device_id_type=MESH)
+    pl.semaphore_wait(barrier, len(peers))
+
+
+def buffer_shapes(rows, cols):
+    half = Region(0, rows, 0, cols).part(0, 2)
+    shapes = [half.shape(), half.shape()]
+    block = half
+    for _ in range(3):
+        block = block.part(0, RING)
+        piece = block.part(0, 2)
+        shapes += [piece.shape(), piece.shape(), block.shape(), block.shape()]
+    return shapes
+
+
+def reduce_unit(here, order, grad, whole, buffers, out, sems, scale):
+    core = here["core"]
+    far = partner(here)
+    from_pair, total = buffers[0], buffers[1]
+    pair = sems.copy(whole.part(1 - core, 2).at(grad), from_pair, far)
+    yield
+    pair.wait_recv()
+    mine = whole.part(core, 2)
+    total[...] = mine.load(grad) + from_pair[...]
+    base = Region(0, mine.rows, 0, mine.cols)
+    levels = []
+    for level, axis in enumerate(order):
+        from_left_far, from_right_far, from_left, from_right = buffers[2 + 4 * level : 6 + 4 * level]
+        at = here[axis]
+        right, left = neighbour(here, axis, 1), neighbour(here, axis, -1)
+        shard = [base.part(lax.rem(at + step, RING), RING) for step in range(RING)]
+        local = Region(0, shard[0].rows, 0, shard[0].cols)
+        first, second = local.part(0, 2), local.part(1, 2)
+        far_right = sems.copy(shard[2].part(0, 2).at(total), from_left_far, right)
+        far_left = sems.copy(shard[2].part(1, 2).at(total), from_right_far, left)
+        near_right = sems.copy(shard[1].part(1, 2).at(total), second.at(from_left), right)
+        near_left = sems.copy(shard[3].part(0, 2).at(total), first.at(from_right), left)
+        yield
+        far_right.wait_recv()
+        block = shard[1].part(0, 2)
+        block.store(total, block.load(total) + from_left_far[...])
+        sum_right = sems.copy(block.at(total), first.at(from_left), right)
+        far_left.wait_recv()
+        block = shard[3].part(1, 2)
+        block.store(total, block.load(total) + from_right_far[...])
+        sum_left = sems.copy(block.at(total), second.at(from_right), left)
+        yield
+        for copy in (near_right, near_left, sum_right, sum_left):
+            copy.wait_recv()
+        result = shard[0].load(total) + (from_left[...] + from_right[...])
+        if level < 2:
+            shard[0].store(total, result)
+        else:
+            shard[0].moved(mine.row, mine.col).store(out, result * scale)
+        levels.append((shard, right, left))
+        base = shard[0]
+    for level in (2, 1, 0):
+        shard, right, left = levels[level]
+        shard = [block.moved(mine.row, mine.col) for block in shard]
+        halves = [(block.part(0, 2).at(out), block.part(1, 2).at(out)) for block in shard]
+        own_first, own_second = halves[0]
+        right_first = sems.copy(own_first, own_first, right)
+        left_second = sems.copy(own_second, own_second, left)
+        right_second = sems.copy(own_second, own_second, right)
+        left_first = sems.copy(own_first, own_first, left)
+        if level == 0:
+            pair_copies = [sems.copy(shard[0].at(out), shard[0].at(out), far)]
+        yield
+        right_first.wait_recv()
+        pass_right = sems.copy(halves[3][0], halves[3][0], right)
+        left_second.wait_recv()
+        pass_left = sems.copy(halves[1][1], halves[1][1], left)
+        yield
+        right_second.wait_recv()
+        left_first.wait_recv()
+        if level == 0:
+            pair_copies += [sems.copy(shard[step].at(out), shard[step].at(out), far) for step in (1, 3)]
+            yield
+        pass_right.wait_recv()
+        pass_left.wait_recv()
+        if level == 0:
+            pair_copies.append(sems.copy(shard[2].at(out), shard[2].at(out), far))
+    yield
+    for copy in pair_copies:
+        copy.wait_recv()
+
+
+COPIES = 1 + 3 * 6 + 3 * 6 + 4
+
+
+def reduce_kernel(scale, *refs):
+    grads, refs = refs[:5], refs[5:]
+    outs, refs = refs[:5], refs[5:]
+    send, recv = refs[-2:]
+    here = place()
+    greet(here)
+    sems = Semaphores(send, recv)
+    running = []
+    at = 0
+    for number, (array, row, rows, cols) in enumerate(UNITS):
+        count = len(buffer_shapes(rows, cols))
+        running.append(
+            reduce_unit(here, ORDERS[number % 3], grads[array], Region(row, rows, 0, cols), refs[at : at + count], outs[array], sems, scale)
+        )
+        at += count
+    while running:
+        for unit in list(running):
+            if next(unit, "done") == "done":
+                running.remove(unit)
+    for copy in sems.copies:
+        copy.wait_send()
+
+
+def all_reduce(grads, scale):
+    scratch = []
+    for _, _, rows, cols in UNITS:
+        scratch += [pltpu.VMEM(shape, jnp.float32) for shape in buffer_shapes(rows, cols)]
+    scratch += [pltpu.SemaphoreType.DMA((COPIES * len(UNITS),))] * 2
+    vmem = pl.BlockSpec(memory_space=pltpu.VMEM)
+
+    def body(*refs):
+        reduce_kernel(scale, *refs)
+
+    return pl.pallas_call(
+        body,
+        out_shape=[jax.ShapeDtypeStruct(shape, jnp.float32) for shape in SHAPES],
+        in_specs=[vmem] * 5,
+        out_specs=[vmem] * 5,
+        scratch_shapes=scratch,
+        compiler_params=pltpu.CompilerParams(collective_id=0, has_side_effects=True, vmem_limit_bytes=48 * 1024 * 1024),
+    )(*grads)
 
 
 def solution(mesh):
@@ -36,9 +254,6 @@
     scale = 1.0 / device_count
     row_spec = P(batch_axes, None)
     full_spec = P(None, None)
-
-    def mean_over_devices(grad):
-        return lax.psum(grad, batch_axes) * scale
 
     def device_step(x_in, g_out, w_in, w_up1, w_down1, w_up2, w_down2):
         x_mid = plain_product(x_in, w_in).astype(jnp.bfloat16)
@@ -47,18 +262,19 @@
         hid_two = (plain_product(act_one, w_down1) + x_mid.astype(jnp.float32)).astype(jnp.bfloat16)
         pre_three = plain_product(hid_two, w_up2).astype(jnp.bfloat16)
         act_three = gelu_value(pre_three).astype(jnp.bfloat16)
-        dw_down2 = mean_over_devices(rows_contract(act_three, g_out))
+        dw_down2 = rows_contract(act_three, g_out)
         d_act3 = times_transposed(g_out, w_down2).astype(jnp.bfloat16)
         d_pre3 = (d_act3.astype(jnp.float32) * gelu_slope(pre_three)).astype(jnp.bfloat16)
-        dw_up2 = mean_over_devices(rows_contract(hid_two, d_pre3))
+        dw_up2 = rows_contract(hid_two, d_pre3)
         d_hid2 = (times_transposed(d_pre3, w_up2) + g_out.astype(jnp.float32)).astype(jnp.bfloat16)
-        dw_down1 = mean_over_devices(rows_contract(act_one, d_hid2))
+        dw_down1 = rows_contract(act_one, d_hid2)
         d_act1 = times_transposed(d_hid2, w_down1).astype(jnp.bfloat16)
         d_pre1 = (d_act1.astype(jnp.float32) * gelu_slope(pre_one)).astype(jnp.bfloat16)
-        dw_up1 = mean_over_devices(rows_contract(x_mid, d_pre1))
+        dw_up1 = rows_contract(x_mid, d_pre1)
         d_mid = (times_transposed(d_pre1, w_up1) + d_hid2.astype(jnp.float32)).astype(jnp.bfloat16)
-        dw_in = mean_over_devices(rows_contract(x_in, d_mid))
+        dw_in = rows_contract(x_in, d_mid)
         dx_rows = times_transposed(d_mid, w_in).astype(jnp.bfloat16)
+        dw_down2, dw_up2, dw_down1, dw_up1, dw_in = all_reduce((dw_down2, dw_up2, dw_down1, dw_up1, dw_in), scale)
         return dx_rows, dw_in, dw_up1, dw_down1, dw_up2, dw_down2
 
     return jax.shard_map(

time: 209 us -> 97.6 us (0.47)
  waiting for transfers between devices: 160 us -> 0 us
  Pallas kernels: 0 us -> 64.6 us
  between operations: 14.2 us -> 0.81 us
  other arithmetic: 6.5 us -> 0 us
  local copies, waits for them, and re-layouts: 3.24 us -> 6.7 us
    psum x1 -> x0, waiting for transfers between devices: 160 us -> none  [mean_over_devices(): return lax.psum(grad, batch_axes) * scale]
    pallas_call x0 -> x1, Pallas kernels: none -> 64.6 us  [all_reduce(): pl.pallas_call(body, out_shape=[jax.ShapeDtypeStruct(shape, jnp.float32)...]
    mul x3 -> x0, other arithmetic: 6.5 us -> none  [mean_over_devices(): return lax.psum(grad, batch_axes) * scale]
    unnamed x19 -> x21, local copies, waits for them, and re-layouts: 3.24 us -> 6.7 us
  transfers between devices with their start and end apart: 1 -> 0, of which waited for: 1 -> 0; matrix products, arithmetic and copies ran while one was open for 2% -> 0% of each run, Pallas kernels for 0% -> 0%
where the time goes in v1:
time: 97.6 us; the launch traced here: 97.4 us
  Pallas kernels  64.6 us (66%)
  matrix products  25.4 us (26%)
  local copies, waits for them, and re-layouts  6.7 us (7%)
    pallas_call x1, Pallas kernels, all_reduce(): pl.pallas_call(body, out_shape=[jax.ShapeDtypeStruct(shape, jnp.float32)...  64.6 us
    dot_general x5, matrix products, rows_contract(): lax.dot_general(first_op, second_op, (((0,), (0,)), ((), ())), preferred_...  10 us
    dot_general x5, matrix products, times_transposed(): lax.dot_general(first_op, second_op, (((1,), (1,)), ((), ())), preferred_...  8.83 us
    unnamed x21, local copies, waits for them, and re-layouts  6.7 us
    dot_general x4, matrix products, plain_product(): lax.dot_general(first_op, second_op, (((1,), (0,)), ((), ())), preferred_...  6.52 us

profile of v1, /device:TPU:1, one launch (start us, length us, event | category | flops | bytes accessed | tf_op | source)
XLA Modules:
  0.0 97.4 jit_solution(4793997968633595207)
XLA Ops:
  0.6 0.0 copy-start
  0.6 0.0 copy-start.2
  0.7 1.2 %copy-done = bf16[2048,256]{1,0:T(8,128)(2,1)S(1)} copy-done((bf16[2048,256]{1,0:T(8,128)(2,1)S(1)}, bf16[2048,256]{1,0:T(8,128)(2,1)}, u32[]{:S(2)}) %copy-start) | copy-done | bytes 1048600
  1.9 3.4 %convolution_convert_fusion.3 = bf16[1024,256]{1,0:T(8,128)(2,1)S(1)} fusion(bf16[1024,2048]{1,0:T(8,128)(2,1)} %param.7, bf16[2048,256]{1,0:T(8,128)(2,1)S(1)} %copy-done), kind=kOutput, calls=%fused_computation.40 | convolution fusion | flops 1074003968 | bytes 5767168 | tf_op jit(solution)/shard_map/dot_general | solution.py:36
  5.3 0.0 copy-done.2
  5.3 0.0 copy-start.4
  5.3 1.6 %fusion.3 = (f32[1024,1024]{1,0:T(8,128)S(1)}, bf16[1024,1024]{1,0:T(8,128)(2,1)S(1)}) fusion(bf16[1024,256]{1,0:T(8,128)(2,1)S(1)} %convolution_convert_fusion.3, bf16[256,1024]{1,0:T(8,128)(2,1)S(1)} %copy-done.2), kind=kOutput, calls=%fused_computation.13 | convolution fusion | flops 541065216 | bytes 7340032 | tf_op jit(solution)/shard_map/dot_general | solution.py:36
  7.0 0.0 copy-start.3
  7.0 0.0 copy-done.4
  7.0 0.0 copy-start.7
  7.0 0.7 fusion.21
  7.7 0.3 copy-done.3
  8.0 0.7 convolution_convert_fusion.1
  8.7 0.0 copy-done.7
  8.7 0.0 copy-start.6
  8.7 1.7 %fusion.18.refs_0_ = f32[1024,256]{1,0:T(8,128)S(1)} fusion(bf16[1024,256]{1,0:T(8,128)(2,1)S(1)} %copy-done.7, bf16[1024,1024]{1,0:T(8,128)(2,1)S(1)} %convolution_convert_fusion.1), kind=kOutput, calls=%fused_computation.30 | convolution fusion | flops 543162368 | bytes 3670016 | tf_op jit(solution)/shard_map/dot_general | solution.py:40
  10.5 0.0 copy-done.6
  10.5 2.4 %fusion.15 = bf16[1024,1024]{1,0:T(8,128)(2,1)S(1)} fusion(bf16[1024,1024]{1,0:T(8,128)(2,1)S(1)} %convolution_convert_fusion.1, bf16[1024,256]{1,0:T(8,128)(2,1)S(1)} %copy-done.7, bf16[1024,256]{1,0:T(8,128)(2,1)S(1)} %copy-done.6), kind=kOutput, calls=%fused_computation.25 | convolution fusion | flops 550502400 | bytes 5242880 | tf_op jit(solution)/shard_map/dot_general | solution.py:44
  12.9 0.8 fusion.22
  13.7 1.7 %fusion.29.refs_1_ = f32[256,1024]{1,0:T(8,128)} fusion(bf16[1024,256]{1,0:T(8,128)(2,1)S(1)} %fusion.21, bf16[1024,1024]{1,0:T(8,128)(2,1)S(1)} %fusion.15), kind=kOutput, calls=%fused_computation.43 | convolution fusion | flops 536870912 | bytes 3670016 | tf_op jit(solution)/shard_map/dot_general | solution.py:40
  15.4 1.8 %fusion.25.refs_2_ = f32[1024,256]{1,0:T(8,128)} fusion(bf16[1024,256]{1,0:T(8,128)(2,1)S(1)} %fusion.22, f32[1024,1024]{1,0:T(8,128)S(1)} %get-tuple-element.16, bf16[1024,1024]{1,0:T(8,128)(2,1)S(1)} %get-tuple-element.17), kind=kOutput, calls=%fused_computation.42 | convolution fusion | flops 541065216 | bytes 7864320 | tf_op jit(solution)/shard_map/dot_general | solution.py:40
  17.2 1.6 %fusion.8 = bf16[1024,1024]{1,0:T(8,128)(2,1)S(1)} fusion(bf16[1024,1024]{1,0:T(8,128)(2,1)S(1)} %get-tuple-element.17, f32[1024,1024]{1,0:T(8,128)S(1)} %get-tuple-element.16, bf16[1024,256]{1,0:T(8,128)(2,1)S(1)} %fusion.22, bf16[1024,256]{1,0:T(8,128)(2,1)S(1)} %copy-done.4), kind=kOutput, calls=%fused_computation.18 | convolution fusion | flops 548405248 | bytes 9437184 | tf_op jit(solution)/shard_map/dot_general | solution.py:44
  18.8 0.0 copy-start.5
  18.8 0.7 fusion.23
  19.6 1.7 %fusion.30.refs_3_ = f32[256,1024]{1,0:T(8,128)} fusion(bf16[1024,256]{1,0:T(8,128)(2,1)S(1)} %convolution_convert_fusion.3, bf16[1024,1024]{1,0:T(8,128)(2,1)S(1)} %fusion.8), kind=kOutput, calls=%fused_computation.44 | convolution fusion | flops 536870912 | bytes 3670016 | tf_op jit(solution)/shard_map/dot_general | solution.py:40
  21.3 0.0 copy-done.5
  21.3 3.1 %convolution_bitcast_fusion.refs_4_ = f32[2048,256]{1,0:T(8,128)} fusion(bf16[1024,256]{1,0:T(8,128)(2,1)S(1)} %fusion.23, bf16[1024,2048]{1,0:T(8,128)(2,1)S(1)} %copy-done.5), kind=kOutput, calls=%fused_computation.29 | convolution fusion | flops 1073741824 | bytes 6815744 | tf_op jit(solution)/shard_map/dot_general | solution.py:40
  24.3 64.6 %shard_map.118 = (f32[1024,256]{1,0:T(8,128)S(1)}, f32[256,1024]{1,0:T(8,128)S(1)}, f32[1024,256]{1,0:T(8,128)S(1)}, f32[256,1024]{1,0:T(8,128)S(1)}, f32[2048,256]{1,0:T(8,128)}) custom-call(f32[1024,256]{1,0:T(8,128)S(1)} %fusion.18.refs_0_, f32[256,1024]{1,0:T(8,128)} %fusion.29.refs_1_, f32[1024,256]{1,0:T(8,128)} %fusion.25.refs_2_, ...), custom_call_target="tpu_custom_call" | custom-call | tf_op jit(solution)/shard_map/pallas_call | solution.py:241
  88.9 0.0 copy-start.1
  88.9 3.3 %convolution_convert_fusion = bf16[1024,2048]{1,0:T(8,128)(2,1)} fusion(bf16[1024,256]{1,0:T(8,128)(2,1)S(1)} %fusion.23, bf16[2048,256]{1,0:T(8,128)(2,1)S(1)} %copy-done), kind=kOutput, calls=%fused_computation.28 | convolution fusion | flops 1075838976 | bytes 5767168 | tf_op jit(solution)/shard_map/dot_general | solution.py:44
  92.2 0.0 copy-done.1
  92.2 1.3 %copy.20 = f32[2048,256]{1,0:T(8,128)} copy(f32[2048,256]{1,0:T(8,128)S(1)} %copy-done.1) | data formatting | bytes 4194304
  93.5 1.0 copy.21
  94.5 1.0 copy.22
  95.5 1.0 copy.23
  96.5 1.0 copy.24
Async XLA Ops:
  0.6 1.2 %copy-start = (bf16[2048,256]{1,0:T(8,128)(2,1)S(1)}, bf16[2048,256]{1,0:T(8,128)(2,1)}, u32[]{:S(2)}) copy-start(bf16[2048,256]{1,0:T(8,128)(2,1)} %param.9) | copy-start | bytes 3145732
  0.6 4.7 %copy-start.2 = (bf16[256,1024]{1,0:T(8,128)(2,1)S(1)}, bf16[256,1024]{1,0:T(8,128)(2,1)}, u32[]{:S(2)}) copy-start(bf16[256,1024]{1,0:T(8,128)(2,1)} %param.10) | copy-start | bytes 1572868
  5.3 1.7 %copy-start.4 = (bf16[1024,256]{1,0:T(8,128)(2,1)S(1)}, bf16[1024,256]{1,0:T(8,128)(2,1)}, u32[]{:S(2)}) copy-start(bf16[1024,256]{1,0:T(8,128)(2,1)} %param.11) | copy-start | bytes 1572868
  7.0 1.0 %copy-start.3 = (bf16[256,1024]{1,0:T(8,128)(2,1)S(1)}, bf16[256,1024]{1,0:T(8,128)(2,1)}, u32[]{:S(2)}) copy-start(bf16[256,1024]{1,0:T(8,128)(2,1)} %param.12) | copy-start | bytes 1572868
  7.0 1.7 %copy-start.7 = (bf16[1024,256]{1,0:T(8,128)(2,1)S(1)}, bf16[1024,256]{1,0:T(8,128)(2,1)}, u32[]{:S(2)}) copy-start(bf16[1024,256]{1,0:T(8,128)(2,1)} %param.8) | copy-start | bytes 1572868
  8.7 1.8 %copy-start.6 = (bf16[1024,256]{1,0:T(8,128)(2,1)S(1)}, bf16[1024,256]{1,0:T(8,128)(2,1)}, u32[]{:S(2)}) copy-start(bf16[1024,256]{1,0:T(8,128)(2,1)} %param.13) | copy-start | bytes 1572868
  18.8 2.5 %copy-start.5 = (bf16[1024,2048]{1,0:T(8,128)(2,1)S(1)}, bf16[1024,2048]{1,0:T(8,128)(2,1)}, u32[]{:S(2)}) copy-start(bf16[1024,2048]{1,0:T(8,128)(2,1)} %param.7) | copy-start | bytes 12582916
  88.9 3.3 %copy-start.1 = (f32[2048,256]{1,0:T(8,128)S(1)}, f32[2048,256]{1,0:T(8,128)}, u32[]{:S(2)}) copy-start(f32[2048,256]{1,0:T(8,128)} %get-tuple-element.25) | copy-start | bytes 6291460

commit v2 on v0

v2 whole, which is shorter than its diff:
```python
import itertools
import math
import jax
import jax.numpy as jnp
from jax import lax
from jax.experimental import pallas as pl
from jax.experimental.pallas import tpu as pltpu
from jax.sharding import PartitionSpec as P

SQRT_HALF = 0.7071067811865476
INV_SQRT_TAU = 0.3989422804014327
MESH = pl.DeviceIdType.MESH
RING = 4
ROWS = 1024
TILE = 512
HALF, WIDE = jnp.bfloat16, jnp.float32
IN, UP1, DOWN1, UP2, DOWN2 = range(5)
SHAPES = ((2048, 256), (256, 1024), (1024, 256), (256, 1024), (1024, 256))
ORDERS = ((("x",), ("y", "z")), (("y",), ("z", "x")), (("z",), ("x", "y")))


def gelu_pair(pre_act):
    wide = pre_act.astype(WIDE)
    share = 0.5 * (1.0 + lax.erf(wide * SQRT_HALF))
    return wide * share, share + wide * jnp.exp(-0.5 * wide * wide) * INV_SQRT_TAU


def plain_product(first_op, second_op):
    return lax.dot_general(first_op, second_op, (((1,), (0,)), ((), ())), preferred_element_type=jnp.float32)


def rows_contract(first_op, second_op):
    return lax.dot_general(first_op, second_op, (((0,), (0,)), ((), ())), preferred_element_type=jnp.float32)


def times_transposed(first_op, second_op):
    return lax.dot_general(first_op, second_op, (((1,), (1,)), ((), ())), preferred_element_type=jnp.float32)


def hinted(value, step):
    return value if isinstance(value, int) else pl.multiple_of(value, step)


class Region:
    def __init__(self, row, rows, col, cols):
        self.row, self.rows, self.col, self.cols = row, rows, col, cols

    def at(self, ref):
        return ref.at[pl.ds(hinted(self.row, 8), self.rows), pl.ds(hinted(self.col, 128), self.cols)]

    def load(self, ref):
        return ref[pl.ds(hinted(self.row, 8), self.rows), pl.ds(hinted(self.col, 128), self.cols)]

    def store(self, ref, value):
        ref[pl.ds(hinted(self.row, 8), self.rows), pl.ds(hinted(self.col, 128), self.cols)] = value

    def part(self, index, count):
        if self.rows // count >= 8:
            step = self.rows // count
            return Region(self.row + index * step, step, self.col, self.cols)
        step = self.cols // count
        if step >= 128:
            return Region(self.row, self.rows, self.col + index * step, step)
        rows, cols = self.rows // 2, self.cols // (count // 2)
        across = self.cols // cols
        return Region(self.row + index // across * rows, rows, self.col + lax.rem(index, across) * cols, cols)

    def shape(self):
        return (self.rows, self.cols)

    def moved(self, row, col):
        return Region(self.row + row, self.rows, self.col + col, self.cols)


class Semaphores:
    def __init__(self, send, recv):
        self.send, self.recv, self.sends, self.recvs, self.closing = send, recv, 0, 0, []

    def stage(self, span):
        number = self.sends
        self.sends += 1
        self.closing.append((number, span))
        return number

    def arrival(self):
        self.recvs += 1
        return self.recvs - 1

    def copy(self, source, target, device, stage, arrival):
        pltpu.make_async_remote_copy(
            src_ref=source,
            dst_ref=target,
            send_sem=self.send.at[stage],
            recv_sem=self.recv.at[arrival],
            device_id=device,
            device_id_type=MESH,
        ).start()

    def arrived(self, arrival, span):
        pltpu.make_async_copy(span, span, self.recv.at[arrival]).wait()

    def close(self):
        for number, span in self.closing:
            pltpu.make_async_copy(span, span, self.send.at[number]).wait()


def place():
    x = lax.axis_index("x")
    return {"x": x // 2, "y": lax.axis_index("y"), "z": lax.axis_index("z"), "core": lax.rem(x, 2)}


def device_at(here, offsets):
    where = {}
    for axis, step in offsets:
        other = lax.rem(here[axis] + step, RING)
        where[axis] = other * 2 + here["core"] if axis == "x" else other
    return where


def partner(here):
    return {"x": here["x"] * 2 + 1 - here["core"]}


def group_offsets(axes):
    steps = list(itertools.product(range(RING), repeat=len(axes)))[1:]
    steps.sort(key=lambda step: -sum(min(s, RING - s) for s in step))
    return steps


def greet(here, groups):
    barrier = pltpu.get_barrier_semaphore()
    peers = {(("core", 1),): partner(here)}
    for axes in groups:
        for step in group_offsets(axes):
            key = tuple(sorted((axis, s) for axis, s in zip(axes, step) if s))
            peers[key] = device_at(here, key)
    for peer in peers.values():
        pl.semaphore_signal(barrier, inc=1, device_id=peer, device_id_type=MESH)
    return len(peers)


def shard_of(block, here, axes, step):
    for axis, s in zip(axes, step):
        block = block.part(lax.rem(here[axis] + s, RING) if s else here[axis], RING)
    return block


def buffer_shapes(half, levels):
    block = half(0)
    shapes = [block.shape(), block.shape()]
    for axes in levels:
        for _ in axes:
            block = block.part(0, RING)
        shapes.append((RING ** len(axes) - 1,) + block.shape())
    return shapes


def reduce_unit(here, levels, grad, half, buffers, out, sems, scale):
    core = here["core"]
    far = partner(here)
    from_pair, total = buffers[0], buffers[1]
    arrival = sems.arrival()
    sems.copy(grad, from_pair, far, sems.stage(from_pair), arrival)
    yield
    sems.arrived(arrival, from_pair)
    mine = half(core)
    total[...] += from_pair[...]
    base = Region(0, mine.rows, 0, mine.cols)
    bases = [base]
    for level, axes in enumerate(levels):
        slots = buffers[2 + level]
        steps = group_offsets(axes)
        stage, arrival = sems.stage(slots), sems.arrival()
        for slot, step in enumerate(steps):
            target = device_at(here, list(zip(axes, step)))
            sems.copy(shard_of(base, here, axes, step).at(total), slots.at[slot], target, stage, arrival)
        yield
        base = shard_of(base, here, axes, (0,) * len(axes))
        bases.append(base)
        sems.arrived(arrival, slots)
        result = base.load(total)
        for slot in range(len(steps)):
            result = result + slots[slot]
        if level + 1 < len(levels):
            base.store(total, result)
        else:
            base.moved(mine.row, mine.col).store(out, result * scale)
    for level in reversed(range(1, len(levels))):
        slots, axes = buffers[2 + level], levels[level]
        own = bases[level + 1].moved(mine.row, mine.col).at(out)
        stage, arrival = sems.stage(slots), sems.arrival()
        for step in group_offsets(axes):
            sems.copy(own, own, device_at(here, list(zip(axes, step))), stage, arrival)
        yield
        sems.arrived(arrival, slots)
    axes = levels[0]
    steps = group_offsets(axes)
    own = bases[1].moved(mine.row, mine.col).at(out)
    stage, arrivals = sems.stage(buffers[2]), [sems.arrival() for _ in steps]
    for step, arrival in zip(steps, arrivals):
        sems.copy(own, own, device_at(here, list(zip(axes, step))), stage, arrival)
    stage, last = sems.stage(from_pair), sems.arrival()
    sems.copy(own, own, far, stage, last)
    yield
    for step, arrival in reversed(list(zip(steps, arrivals))):
        back = tuple((RING - s) % RING for s in step)
        block = shard_of(bases[0], here, axes, back).moved(mine.row, mine.col).at(out)
        sems.arrived(arrival, block)
        sems.copy(block, block, far, stage, last)
    yield
    sems.arrived(last, from_pair)


def stages_of(levels):
    return 2 + 2 * len(levels)


def arrivals_of(levels):
    return stages_of(levels) - 1 + RING ** len(levels[0]) - 1


def tall(row, rows, apart):
    return lambda core: Region(row + core * apart, rows, 0, 256)


def wide(row, rows):
    return lambda core: Region(row, rows, core * 512, 512)


UNITS = (
    (DOWN2, tall(0, 512, 512), ORDERS[0]),
    (UP2, wide(0, 256), ORDERS[1]),
    (DOWN1, tall(0, 512, 512), ORDERS[2]),
    (UP1, wide(0, 256), ORDERS[0]),
    (IN, tall(0, 512, 1024), ORDERS[1]),
    (IN, tall(512, 512, 1024), ORDERS[2]),
)
PLAN = (
    "c0", "c1", "c2", "c3", "bar", "o0", "u0", "m0", "c4", "o1", "u1", "m1",
    "u0", "c5", "o2", "u2", "m2", "u1", "c6", "u2", "o3", "u3", "m3", "c7",
    "u3", "o4", "u4", "o5", "u5", "m4", "m5", "c8", "u4", "u5",
)


def tiles():
    return [pl.ds(at, TILE) for at in range(0, ROWS, TILE)]


def step_kernel(scale, *refs):
    inputs, refs = refs[:7], refs[7:]
    dx, *outs = refs[:6]
    refs = refs[6:]
    x, g, w_in, w_up1, w_down1, w_up2, w_down2 = refs[:7]
    refs = refs[7:]
    mid, act_one, slope_one, hid_two, act_three, slope_three, d_pre3, d_hid2, d_pre1, d_mid = refs[:10]
    refs = refs[10:]
    grads, refs = refs[: len(UNITS)], refs[len(UNITS) :]
    buffers, (loads, send, recv) = refs[:-3], refs[-3:]
    here = place()
    peers = greet(here, sorted({axes for _, _, levels in UNITS for axes in levels}))

    pending = {}
    number = 0
    for name, source, target in zip(("x", "g", "w_in", "w_up1", "w_down1", "w_up2", "w_down2"), inputs, refs_of(x, g, w_in, w_up1, w_down1, w_up2, w_down2)):
        pending[name] = []
        blocks = tiles() if name == "x" else [pl.ds(0, target.shape[0])]
        for block in blocks:
            pending[name].append(pltpu.make_async_copy(source.at[block], target.at[block], loads.at[number]))
            number += 1
    for name in ("w_in", "x", "w_up1", "w_down1", "w_up2", "g", "w_down2"):
        for copy in pending[name]:
            copy.start()

    def ready(name):
        for copy in pending.pop(name, []):
            copy.wait()

    def project():
        ready("w_in")
        for copy, rows in zip(pending.pop("x"), tiles()):
            copy.wait()
            mid[rows, :] = plain_product(x[rows, :], w_in[...]).astype(HALF)

    def expand(source, weight, name, act, slope):
        ready(name)
        for rows in tiles():
            value, rate = gelu_pair(plain_product(source[rows, :], weight[...]).astype(HALF))
            act[rows, :] = value.astype(HALF)
            slope[rows, :] = rate

    def second():
        ready("w_down1")
        for rows in tiles():
            hid_two[rows, :] = (plain_product(act_one[rows, :], w_down1[...]) + mid[rows, :].astype(WIDE)).astype(HALF)

    def before_gelu(source, weight, slope, target):
        for rows in tiles():
            grad = times_transposed(source[rows, :], weight[...]).astype(HALF)
            target[rows, :] = (grad.astype(WIDE) * slope[rows, :]).astype(HALF)

    def before_layer(source, weight, skip, target):
        for rows in tiles():
            target[rows, :] = (times_transposed(source[rows, :], weight[...]) + skip[rows, :].astype(WIDE)).astype(HALF)

    def third():
        expand(hid_two, w_up2, "w_up2", act_three, slope_three)
        ready("g")
        ready("w_down2")

    def leave():
        for rows in tiles():
            dx[rows, :] = times_transposed(d_mid[rows, :], w_in[...]).astype(HALF)

    stages = (
        project,
        lambda: expand(mid, w_up1, "w_up1", act_one, slope_one),
        second,
        third,
        lambda: before_gelu(g, w_down2, slope_three, d_pre3),
        lambda: before_layer(d_pre3, w_up2, g, d_hid2),
        lambda: before_gelu(d_hid2, w_down1, slope_one, d_pre1),
        lambda: before_layer(d_pre1, w_up1, d_hid2, d_mid),
        leave,
    )
    factors = {DOWN2: (act_three, g), UP2: (hid_two, d_pre3), DOWN1: (act_one, d_hid2), UP1: (mid, d_pre1), IN: (x, d_mid)}

    def gradient(unit, core):
        array, half, _ = UNITS[unit]
        first, other = factors[array]
        block = half(core)
        left = first[:, pl.ds(hinted(block.row, 128), block.rows)]
        right = other[:, pl.ds(hinted(block.col, 128), block.cols)]
        piece = rows_contract(left, right)
        if core is here["core"]:
            totals[unit][...] = piece
        else:
            grads[unit][...] = piece

    sems = Semaphores(send, recv)
    units, totals = [], []
    at = 0
    for array, half, levels in UNITS:
        count = len(buffer_shapes(half, levels))
        units.append(reduce_unit(here, levels, grads[len(units)], half, buffers[at : at + count], outs[array], sems, scale))
        totals.append(buffers[at + 1])
        at += count
    live = dict(enumerate(units))

    def advance(unit):
        if unit in live and next(live[unit], "done") == "done":
            del live[unit]

    for word in PLAN:
        if word == "bar":
            pl.semaphore_wait(pltpu.get_barrier_semaphore(), peers)
            continue
        kind, which = word[0], int(word[1:])
        if kind == "c":
            stages[which]()
        elif kind == "u":
            advance(which)
        else:
            gradient(which, 1 - here["core"] if kind == "o" else here["core"])
    for name in list(pending):
        ready(name)
    while live:
        for unit in list(live):
            advance(unit)
    sems.close()


def refs_of(*refs):
    return refs


def fused_step(args, scale):
    vmem = pltpu.VMEM
    inputs = ((ROWS, 2048), (ROWS, 256), (2048, 256), (256, 1024), (1024, 256), (256, 1024), (1024, 256))
    scratch = [vmem(shape, HALF) for shape in inputs]
    scratch += [
        vmem((ROWS, 256), HALF),
        vmem((ROWS, 1024), HALF),
        vmem((ROWS, 1024), WIDE),
        vmem((ROWS, 256), HALF),
        vmem((ROWS, 1024), HALF),
        vmem((ROWS, 1024), WIDE),
        vmem((ROWS, 1024), HALF),
        vmem((ROWS, 256), HALF),
        vmem((ROWS, 1024), HALF),
        vmem((ROWS, 256), HALF),
    ]
    scratch += [vmem(half(0).shape(), WIDE) for _, half, _ in UNITS]
    for _, half, levels in UNITS:
        scratch += [vmem(shape, WIDE) for shape in buffer_shapes(half, levels)]
    scratch += [pltpu.SemaphoreType.DMA((6 + ROWS // TILE,))]
    scratch += [pltpu.SemaphoreType.DMA((sum(count(levels) for _, _, levels in UNITS),)) for count in (stages_of, arrivals_of)]
    outs = [jax.ShapeDtypeStruct((ROWS, 2048), HALF)] + [jax.ShapeDtypeStruct(shape, WIDE) for shape in SHAPES]

    def body(*refs):
        step_kernel(scale, *refs)

    return pl.pallas_call(
        body,
        out_shape=outs,
        in_specs=[pl.BlockSpec(memory_space=pltpu.HBM)] * 7,
        out_specs=[pl.BlockSpec(memory_space=pltpu.VMEM)] * 6,
        scratch_shapes=scratch,
        compiler_params=pltpu.CompilerParams(collective_id=0, has_side_effects=True, vmem_limit_bytes=40 * 1024 * 1024),
    )(*args)


def deliver(arrays):
    count = len(arrays)

    def body(*refs):
        copies = [pltpu.make_async_copy(refs[i], refs[count + i], refs[-1].at[i]) for i in range(count)]
        for copy in copies:
            copy.start()
        for copy in copies:
            copy.wait()

    return pl.pallas_call(
        body,
        out_shape=[jax.ShapeDtypeStruct(array.shape, array.dtype) for array in arrays],
        in_specs=[pl.BlockSpec(memory_space=pl.ANY)] * count,
        out_specs=[pl.BlockSpec(memory_space=pl.ANY)] * count,
        scratch_shapes=[pltpu.SemaphoreType.DMA((count,))],
        compiler_params=pltpu.CompilerParams(vmem_limit_bytes=1024 * 1024),
    )(*arrays)


def solution(mesh):
    batch_axes = ("z", "y", "x")
    scale = 1.0 / math.prod(mesh.shape.values())
    row_spec = P(batch_axes, None)
    full_spec = P(None, None)

    def device_step(*args):
        args = [pltpu.with_memory_space_constraint(arg, pltpu.HBM) for arg in args]
        return tuple(deliver(fused_step(args, scale)))

    return jax.shard_map(
        device_step,
        mesh=mesh,
        in_specs=(row_spec, row_spec, full_spec, full_spec, full_spec, full_spec, full_spec),
        out_specs=(row_spec, full_spec, full_spec, full_spec, full_spec, full_spec),
        check_vma=False,
    )
```

time: 209 us -> 66.2 us (0.32)
  waiting for transfers between devices: 160 us -> 0 us
  Pallas kernels: 0 us -> 65.3 us
  matrix products: 25.1 us -> 0 us
  between operations: 14.2 us -> 0.8 us
  other arithmetic: 6.5 us -> 0 us
  local copies, waits for them, and re-layouts: 3.24 us -> 0 us
    psum x1 -> x0, waiting for transfers between devices: 160 us -> none  [mean_over_devices(): return lax.psum(grad, batch_axes) * scale]
    pallas_call x0 -> x2, Pallas kernels: none -> 65.3 us  [the longest x1 61.3 us: fused_step(): pl.pallas_call(body, out_shape=outs, in_specs=[pl.BlockSpec(memory_space=...]
    dot_general x14 -> x0, matrix products: 25.1 us -> none  [the longest x5 9.93 us: rows_contract(): lax.dot_general(first_op, second_op, (((0,), (0,)), ((), ())), preferred_...]
    mul x3 -> x0, other arithmetic: 6.5 us -> none  [mean_over_devices(): return lax.psum(grad, batch_axes) * scale]
    unnamed x19 -> x0, local copies, waits for them, and re-layouts: 3.24 us -> none
  transfers between devices with their start and end apart: 1 -> 0, of which waited for: 1 -> 0; matrix products, arithmetic and copies ran while one was open for 2% -> 0% of each run, Pallas kernels for 0% -> 0%
where the time goes in v2:
time: 66.2 us; the launch traced here: 66.1 us
  Pallas kernels  65.3 us (99%)
  between operations  0.8 us (1%)
    pallas_call x1, Pallas kernels, fused_step(): pl.pallas_call(body, out_shape=outs, in_specs=[pl.BlockSpec(memory_space=...  61.3 us
    pallas_call x1, Pallas kernels, deliver(): pl.pallas_call(body, out_shape=[jax.ShapeDtypeStruct(array.shape, array.d...  3.98 us

profile of v2, /device:TPU:1, one launch (start us, length us, event | category | flops | bytes accessed | tf_op | source)
XLA Modules:
  0.0 66.1 jit_solution(12918742295097895703)
XLA Ops:
  0.6 61.3 %shard_map.118 = (bf16[1024,2048]{1,0:T(8,128)(2,1)S(1)}, f32[2048,256]{1,0:T(8,128)S(1)}, f32[256,1024]{1,0:T(8,128)S(1)}, f32[1024,256]{1,0:T(8,128)S(1)}, f32...) custom-call(bf16[1024,2048]{1,0:T(8,128)(2,1)} %refs_0_.1, bf16[1024,256]{1,0:T(8,128)(2,1)} %refs_1_.1, ...), custom_call_target="tpu_custom_call" | custom-call | tf_op jit(solution)/shard_map/pallas_call | solution.py:402
  61.9 4.0 %shard_map.119 = (bf16[1024,2048]{1,0:T(8,128)(2,1)}, f32[2048,256]{1,0:T(8,128)}, f32[256,1024]{1,0:T(8,128)}, f32[1024,256]{1,0:T(8,128)}, f32[256,1024]{1,0:T(8,128)}, /*index=5*/f32[1024,256]{1,0:T(8,128)}) custom-call(bf16[1024,2048]{1,0:T(8,128)(2,1)S(1)} %get-tuple-element.12.refs_0_, f32[2048,256]{1,0:T(8,128)S(1)} %get-tuple-element.13.refs_1_, ...), custom_call_target="tpu_custom_call" | custom-call | tf_op jit(solution)/shard_map/pallas_call | solution.py:422

commit v3 on v2

--- a/solution.py
+++ b/solution.py
@@ -231,14 +231,18 @@
     (DOWN2, tall(0, 512, 512), ORDERS[0]),
     (UP2, wide(0, 256), ORDERS[1]),
     (DOWN1, tall(0, 512, 512), ORDERS[2]),
-    (UP1, wide(0, 256), ORDERS[0]),
-    (IN, tall(0, 512, 1024), ORDERS[1]),
-    (IN, tall(512, 512, 1024), ORDERS[2]),
+    (UP1, wide(0, 128), ORDERS[1]),
+    (UP1, wide(128, 128), ORDERS[2]),
+    (IN, tall(0, 512, 1024), ORDERS[0]),
+    (IN, tall(512, 256, 1024), ORDERS[1]),
+    (IN, tall(768, 256, 1024), ORDERS[2]),
 )
+
 PLAN = (
     "c0", "c1", "c2", "c3", "bar", "o0", "u0", "m0", "c4", "o1", "u1", "m1",
-    "u0", "c5", "o2", "u2", "m2", "u1", "c6", "u2", "o3", "u3", "m3", "c7",
-    "u3", "o4", "u4", "o5", "u5", "m4", "m5", "c8", "u4", "u5",
+    "u0", "c5", "o2", "u2", "m2", "u1", "c6", "u2", "o3", "u3", "o4", "u4",
+    "m3", "m4", "c7", "u3", "u4", "o5", "u5", "o6", "u6", "o7", "u7", "m5",
+    "m6", "m7", "c8", "u5", "u6", "u7",
 )
 
 
@@ -259,37 +263,33 @@
     here = place()
     peers = greet(here, sorted({axes for _, _, levels in UNITS for axes in levels}))
 
-    pending = {}
+    core = here["core"]
+    order = (1 - core, core)
     number = 0
-    for name, source, target in zip(("x", "g", "w_in", "w_up1", "w_down1", "w_up2", "w_down2"), inputs, refs_of(x, g, w_in, w_up1, w_down1, w_up2, w_down2)):
-        pending[name] = []
-        blocks = tiles() if name == "x" else [pl.ds(0, target.shape[0])]
-        for block in blocks:
-            pending[name].append(pltpu.make_async_copy(source.at[block], target.at[block], loads.at[number]))
+    pending = []
+    for source, target, axis in zip(inputs, refs_of(x, g, w_in, w_up1, w_down1, w_up2, w_down2), (1, None, 0, 1, 0, 1, 0)):
+        size = target.shape[axis or 0] // (1 if axis is None else 2)
+        for place_here, place_there in enumerate((0,) if axis is None else order):
+            there, to = pl.ds(hinted(place_there * size, size), size), pl.ds(place_here * size, size)
+            where = (there, to) if axis != 1 else ((slice(None), there), (slice(None), to))
+            pending.append(pltpu.make_async_copy(source.at[where[0]], target.at[where[1]], loads.at[number]))
             number += 1
-    for name in ("w_in", "x", "w_up1", "w_down1", "w_up2", "g", "w_down2"):
-        for copy in pending[name]:
-            copy.start()
-
-    def ready(name):
-        for copy in pending.pop(name, []):
+    for copy in pending:
+        copy.start()
+
+    def project():
+        for copy in pending:
             copy.wait()
-
-    def project():
-        ready("w_in")
-        for copy, rows in zip(pending.pop("x"), tiles()):
-            copy.wait()
+        for rows in tiles():
             mid[rows, :] = plain_product(x[rows, :], w_in[...]).astype(HALF)
 
-    def expand(source, weight, name, act, slope):
-        ready(name)
+    def expand(source, weight, act, slope):
         for rows in tiles():
             value, rate = gelu_pair(plain_product(source[rows, :], weight[...]).astype(HALF))
             act[rows, :] = value.astype(HALF)
             slope[rows, :] = rate
 
     def second():
-        ready("w_down1")
         for rows in tiles():
             hid_two[rows, :] = (plain_product(act_one[rows, :], w_down1[...]) + mid[rows, :].astype(WIDE)).astype(HALF)
 
@@ -303,17 +303,17 @@
             target[rows, :] = (times_transposed(source[rows, :], weight[...]) + skip[rows, :].astype(WIDE)).astype(HALF)
 
     def third():
-        expand(hid_two, w_up2, "w_up2", act_three, slope_three)
-        ready("g")
-        ready("w_down2")
+        expand(hid_two, w_up2, act_three, slope_three)
 
     def leave():
-        for rows in tiles():
-            dx[rows, :] = times_transposed(d_mid[rows, :], w_in[...]).astype(HALF)
+        for place_here, place_there in enumerate(order):
+            columns = pl.ds(hinted(place_there * 1024, 1024), 1024)
+            for rows in tiles():
+                dx[rows, columns] = times_transposed(d_mid[rows, :], w_in[pl.ds(place_here * 1024, 1024), :]).astype(HALF)
 
     stages = (
         project,
-        lambda: expand(mid, w_up1, "w_up1", act_one, slope_one),
+        lambda: expand(mid, w_up1, act_one, slope_one),
         second,
         third,
         lambda: before_gelu(g, w_down2, slope_three, d_pre3),
@@ -324,17 +324,13 @@
     )
     factors = {DOWN2: (act_three, g), UP2: (hid_two, d_pre3), DOWN1: (act_one, d_hid2), UP1: (mid, d_pre1), IN: (x, d_mid)}
 
-    def gradient(unit, core):
+    def gradient(unit, own):
         array, half, _ = UNITS[unit]
         first, other = factors[array]
-        block = half(core)
-        left = first[:, pl.ds(hinted(block.row, 128), block.rows)]
-        right = other[:, pl.ds(hinted(block.col, 128), block.cols)]
-        piece = rows_contract(left, right)
-        if core is here["core"]:
-            totals[unit][...] = piece
-        else:
-            grads[unit][...] = piece
+        block = half(own)
+        left = first[:, block.row : block.row + block.rows]
+        right = other[:, block.col : block.col + block.cols]
+        (totals if own else grads)[unit][...] = rows_contract(left, right)
 
     sems = Semaphores(send, recv)
     units, totals = [], []
@@ -360,9 +356,7 @@
         elif kind == "u":
             advance(which)
         else:
-            gradient(which, 1 - here["core"] if kind == "o" else here["core"])
-    for name in list(pending):
-        ready(name)
+            gradient(which, 0 if kind == "o" else 1)
     while live:
         for unit in list(live):
             advance(unit)
@@ -392,7 +386,7 @@
     scratch += [vmem(half(0).shape(), WIDE) for _, half, _ in UNITS]
     for _, half, levels in UNITS:
         scratch += [vmem(shape, WIDE) for shape in buffer_shapes(half, levels)]
-    scratch += [pltpu.SemaphoreType.DMA((6 + ROWS // TILE,))]
+    scratch += [pltpu.SemaphoreType.DMA((13,))]
     scratch += [pltpu.SemaphoreType.DMA((sum(count(levels) for _, _, levels in UNITS),)) for count in (stages_of, arrivals_of)]
     outs = [jax.ShapeDtypeStruct((ROWS, 2048), HALF)] + [jax.ShapeDtypeStruct(shape, WIDE) for shape in SHAPES]
 

time: 66.2 us -> 64.4 us (0.973)
  Pallas kernels: 65.3 us -> 63.5 us
    pallas_call x1, Pallas kernels: 61.3 us -> 59.5 us  [fused_step(): pl.pallas_call(body, out_shape=outs, in_specs=[pl.BlockSpec(memory_space=...]
where the time goes in v3:
time: 64.4 us; the launch traced here: 64.3 us
  Pallas kernels  63.5 us (99%)
  between operations  0.8 us (1%)
    pallas_call x1, Pallas kernels, fused_step(): pl.pallas_call(body, out_shape=outs, in_specs=[pl.BlockSpec(memory_space=...  59.5 us
    pallas_call x1, Pallas kernels, deliver(): pl.pallas_call(body, out_shape=[jax.ShapeDtypeStruct(array.shape, array.d...  3.98 us

profile of v3, /device:TPU:1, one launch (start us, length us, event | category | flops | bytes accessed | tf_op | source)
XLA Modules:
  0.0 64.3 jit_solution(4458151758758231564)
XLA Ops:
  0.6 59.5 %shard_map.118 = (bf16[1024,2048]{1,0:T(8,128)(2,1)S(1)}, f32[2048,256]{1,0:T(8,128)S(1)}, f32[256,1024]{1,0:T(8,128)S(1)}, f32[1024,256]{1,0:T(8,128)S(1)}, f32...) custom-call(bf16[1024,2048]{1,0:T(8,128)(2,1)} %refs_0_.1, bf16[1024,256]{1,0:T(8,128)(2,1)} %refs_1_.1, ...), custom_call_target="tpu_custom_call" | custom-call | tf_op jit(solution)/shard_map/pallas_call | solution.py:396
  60.2 4.0 %shard_map.119 = (bf16[1024,2048]{1,0:T(8,128)(2,1)}, f32[2048,256]{1,0:T(8,128)}, f32[256,1024]{1,0:T(8,128)}, f32[1024,256]{1,0:T(8,128)}, f32[256,1024]{1,0:T(8,128)}, /*index=5*/f32[1024,256]{1,0:T(8,128)}) custom-call(bf16[1024,2048]{1,0:T(8,128)(2,1)S(1)} %get-tuple-element.12.refs_0_, f32[2048,256]{1,0:T(8,128)S(1)} %get-tuple-element.13.refs_1_, ...), custom_call_target="tpu_custom_call" | custom-call | tf_op jit(solution)/shard_map/pallas_call | solution.py:416

commit v4 on v3

--- a/solution.py
+++ b/solution.py
@@ -240,8 +240,8 @@
 
 PLAN = (
     "c0", "c1", "c2", "c3", "bar", "o0", "u0", "m0", "c4", "o1", "u1", "m1",
-    "u0", "c5", "o2", "u2", "m2", "u1", "c6", "u2", "o3", "u3", "o4", "u4",
-    "m3", "m4", "c7", "u3", "u4", "o5", "u5", "o6", "u6", "o7", "u7", "m5",
+    "c5", "u0", "o2", "u2", "m2", "c6", "u1", "o3", "u3", "o4", "u4", "m3",
+    "m4", "u2", "c7", "o5", "u5", "o6", "u6", "o7", "u7", "u3", "u4", "m5",
     "m6", "m7", "c8", "u5", "u6", "u7",
 )
 

time: 64.4 us -> 63.8 us (level)
  no operation moved by 1% of the time
where the time goes in v4:
time: 63.8 us; the launch traced here: 63.7 us
  Pallas kernels  62.9 us (99%)
  between operations  0.8 us (1%)
    pallas_call x1, Pallas kernels, fused_step(): pl.pallas_call(body, out_shape=outs, in_specs=[pl.BlockSpec(memory_space=...  58.9 us
    pallas_call x1, Pallas kernels, deliver(): pl.pallas_call(body, out_shape=[jax.ShapeDtypeStruct(array.shape, array.d...  3.98 us

profile of v4, /device:TPU:1, one launch (start us, length us, event | category | flops | bytes accessed | tf_op | source)
XLA Modules:
  0.0 63.7 jit_solution(146492986848477198)
XLA Ops:
  0.6 58.9 %shard_map.118 = (bf16[1024,2048]{1,0:T(8,128)(2,1)S(1)}, f32[2048,256]{1,0:T(8,128)S(1)}, f32[256,1024]{1,0:T(8,128)S(1)}, f32[1024,256]{1,0:T(8,128)S(1)}, f32...) custom-call(bf16[1024,2048]{1,0:T(8,128)(2,1)} %refs_0_.1, bf16[1024,256]{1,0:T(8,128)(2,1)} %refs_1_.1, ...), custom_call_target="tpu_custom_call" | custom-call | tf_op jit(solution)/shard_map/pallas_call | solution.py:396
  59.6 4.0 %shard_map.119 = (bf16[1024,2048]{1,0:T(8,128)(2,1)}, f32[2048,256]{1,0:T(8,128)}, f32[256,1024]{1,0:T(8,128)}, f32[1024,256]{1,0:T(8,128)}, f32[256,1024]{1,0:T(8,128)}, /*index=5*/f32[1024,256]{1,0:T(8,128)}) custom-call(bf16[1024,2048]{1,0:T(8,128)(2,1)S(1)} %get-tuple-element.12.refs_0_, f32[2048,256]{1,0:T(8,128)S(1)} %get-tuple-element.13.refs_1_, ...), custom_call_target="tpu_custom_call" | custom-call | tf_op jit(solution)/shard_map/pallas_call | solution.py:416

commit v5 on v4

--- a/solution.py
+++ b/solution.py
@@ -240,8 +240,8 @@
 
 PLAN = (
     "c0", "c1", "c2", "c3", "bar", "o0", "u0", "m0", "c4", "o1", "u1", "m1",
-    "c5", "u0", "o2", "u2", "m2", "c6", "u1", "o3", "u3", "o4", "u4", "m3",
-    "m4", "u2", "c7", "o5", "u5", "o6", "u6", "o7", "u7", "u3", "u4", "m5",
+    "c5", "u0", "o2", "u2", "m2", "c6", "u1", "o3", "o4", "u3", "u4", "m3",
+    "m4", "u2", "c7", "u3", "u4", "o5", "u5", "o6", "u6", "o7", "u7", "m5",
     "m6", "m7", "c8", "u5", "u6", "u7",
 )
 

time: 63.8 us -> 63.2 us (level)
    pallas_call x1, Pallas kernels: 58.9 us -> 58.3 us  [fused_step(): pl.pallas_call(body, out_shape=outs, in_specs=[pl.BlockSpec(memory_space=...]
where the time goes in v5:
time: 63.2 us; the launch traced here: 63.1 us
  Pallas kernels  62.3 us (99%)
  between operations  0.8 us (1%)
    pallas_call x1, Pallas kernels, fused_step(): pl.pallas_call(body, out_shape=outs, in_specs=[pl.BlockSpec(memory_space=...  58.3 us
    pallas_call x1, Pallas kernels, deliver(): pl.pallas_call(body, out_shape=[jax.ShapeDtypeStruct(array.shape, array.d...  3.98 us

profile of v5, /device:TPU:1, one launch (start us, length us, event | category | flops | bytes accessed | tf_op | source)
XLA Modules:
  0.0 63.1 jit_solution(2497172630525728102)
XLA Ops:
  0.6 58.3 %shard_map.118 = (bf16[1024,2048]{1,0:T(8,128)(2,1)S(1)}, f32[2048,256]{1,0:T(8,128)S(1)}, f32[256,1024]{1,0:T(8,128)S(1)}, f32[1024,256]{1,0:T(8,128)S(1)}, f32...) custom-call(bf16[1024,2048]{1,0:T(8,128)(2,1)} %refs_0_.1, bf16[1024,256]{1,0:T(8,128)(2,1)} %refs_1_.1, ...), custom_call_target="tpu_custom_call" | custom-call | tf_op jit(solution)/shard_map/pallas_call | solution.py:396
  58.9 4.0 %shard_map.119 = (bf16[1024,2048]{1,0:T(8,128)(2,1)}, f32[2048,256]{1,0:T(8,128)}, f32[256,1024]{1,0:T(8,128)}, f32[1024,256]{1,0:T(8,128)}, f32[256,1024]{1,0:T(8,128)}, /*index=5*/f32[1024,256]{1,0:T(8,128)}) custom-call(bf16[1024,2048]{1,0:T(8,128)(2,1)S(1)} %get-tuple-element.12.refs_0_, f32[2048,256]{1,0:T(8,128)S(1)} %get-tuple-element.13.refs_1_, ...), custom_call_target="tpu_custom_call" | custom-call | tf_op jit(solution)/shard_map/pallas_call | solution.py:416
